TPU v7x, 128 devices: a whole 4x4x4 slice. The times are simulated.
128 devices in a mesh: gx: 4 (over z), gy: 32 (over y, x, core).
Axes of the slice: x: 4, y: 4, z: 4, core: 2. Of those that a mesh axis runs over, the one named last changes fastest.
Arguments:
- radiance: bfloat16 [8192, 16, 128], P(('gx', 'gy')), may hold values from 0.049804688 to 2
- emission: float32 [8192, 16, 128], P(('gx', 'gy')), may hold values from 0.01 to 1
- reflectance: float32 [8192, 16, 128], P(('gx', 'gy')), may hold values from 0.1 to 0.9
- patch_area: float32 [8192, 128], P(('gx', 'gy')), may hold values from 0.25 to 4
- form_factor: bfloat16 [65536, 128, 128], P(('gx', 'gy')), may hold values from 0.00049972534 to 0.014953613
- source_index: int32 [128, 512], P(('gx', 'gy')), may hold values from 0 to 63
- target_index: int32 [128, 512], P(('gx', 'gy')), may hold values from 0 to 63
- block_index: int32 [128, 512], P(('gx', 'gy')), may hold values from 0 to 511, each once within a row
- valid_count: int32 [128, 128], P(('gx', 'gy')), may hold values from 0 to 4, as said below
Outputs:
- new_radiance: float32 [8192, 16, 128], P(('gx', 'gy'))
Inputs may be any that keep to these rules, and one draw needn't show every extreme that they name: `valid_count`: entry [d, p] is the number of live slots among the 4 slots of device d toward peer p, the live ones first; every row has an entry equal to 4. `block_index`: each row is a permutation of 0 to 511.
All inputs are finite; a program needn't handle non-finite values.
Results may differ from a plain program's by a relative error of at most 0.0012.
Values may be sent and summed in bfloat16 or wider, within the bound.
A program may use at most 128 MiB of HBM per device.

v0:
```python
import jax
import jax.numpy as jnp
from jax import lax
from jax.sharding import PartitionSpec as P


def cut_along(value, dim, peers):
    before, after = (value.shape[:dim], value.shape[dim + 1 :])
    return jnp.moveaxis(value.reshape(*before, peers, -1, *after), dim, 0)


def edges_of(length, count):
    lap = length // count
    if lap >= 8:
        lap -= lap % 8
    return [lap * k for k in range(1, count)]


def in_order(pieces, dim):
    lengths = list(pieces.shape[1:])
    lengths[dim] *= pieces.shape[0]
    return jnp.moveaxis(pieces, 0, dim).reshape(lengths)


def several_exchanges(value, axis, pieces, split_dim, concat_dim):
    blocks = cut_along(value, split_dim, lax.axis_size(axis))
    cut = max(range(1, max(2, blocks.ndim - 1)), key=lambda d: blocks.shape[d])
    outs = []
    for piece in jnp.split(blocks, edges_of(blocks.shape[cut], pieces), axis=cut):
        if piece.size:
            outs.append(lax.all_to_all(piece, axis, split_axis=0, concat_axis=0, tiled=True))
    return in_order(jnp.concatenate(outs, axis=cut), concat_dim)


def shards(
    radiance,
    emission,
    reflectance,
    patch_area,
    form_factor,
    source_index,
    target_index,
    block_index,
    valid_count,
):
    peers = lax.axis_size(("gx", "gy"))
    clusters = radiance.shape[0]
    bands = radiance.shape[1]
    patches = radiance.shape[2]
    link_count = source_index.shape[1]
    slot_count = link_count // peers
    wanted_rows = source_index[0].reshape(peers, slot_count)
    asked_rows = lax.all_to_all(wanted_rows, ("gx", "gy"), split_axis=0, concat_axis=0, tiled=True)
    served = radiance[asked_rows]
    fetched = several_exchanges(served, ("gx", "gy"), 2, 0, 0)
    fetched = fetched.reshape(link_count, bands, patches)
    position = jnp.arange(link_count, dtype=jnp.int32)
    block_row = block_index[0]
    stored_link = jnp.zeros((link_count,), jnp.int32).at[block_row].set(position)
    live_count = valid_count[0]
    live_link = (position % slot_count < live_count[position // slot_count]).astype(jnp.float32)
    live_stored = live_link[stored_link]
    target_stored = target_index[0][stored_link]
    rad_stored = fetched[stored_link]
    forward = jnp.einsum(
        "mij,mbj->mbi", form_factor, rad_stored, preferred_element_type=jnp.float32
    )
    cluster_ids = jnp.arange(clusters, dtype=jnp.int32)
    target_table = (cluster_ids[:, None] == target_stored[None, :]).astype(
        jnp.float32
    ) * live_stored[None, :]
    gathered = jnp.dot(
        target_table,
        forward.reshape(link_count, bands * patches),
        precision=lax.Precision.HIGHEST,
        preferred_element_type=jnp.float32,
    )
    weighted = (patch_area[:, None, :] * radiance.astype(jnp.float32)).astype(jnp.bfloat16)
    weighted_stored = weighted[target_stored]
    backward = jnp.einsum(
        "mij,mbi->mbj", form_factor, weighted_stored, preferred_element_type=jnp.float32
    )
    backward = (backward * live_stored[:, None, None]).astype(jnp.bfloat16)
    backward_links = backward[block_row]
    arrived = lax.all_to_all(
        backward_links.reshape(peers, slot_count, bands, patches),
        ("gx", "gy"),
        split_axis=0,
        concat_axis=0,
        tiled=True,
    )
    arrived = arrived.reshape(link_count, bands * patches).astype(jnp.float32)
    source_table = (cluster_ids[:, None] == asked_rows.reshape(link_count)[None, :]).astype(
        jnp.float32
    )
    returned = jnp.dot(
        source_table, arrived, precision=lax.Precision.HIGHEST, preferred_element_type=jnp.float32
    )
    irradiance = (
        gathered.reshape(clusters, bands, patches)
        + returned.reshape(clusters, bands, patches) / patch_area[:, None, :]
    )
    return emission + reflectance * irradiance


def solution(mesh):
    in_specs = (
        P(("gx", "gy"), None, None),
        P(("gx", "gy"), None, None),
        P(("gx", "gy"), None, None),
        P(("gx", "gy"), None),
        P(("gx", "gy"), None, None),
        P(("gx", "gy"), None),
        P(("gx", "gy"), None),
        P(("gx", "gy"), None),
        P(("gx", "gy"), None),
    )
    out_specs = P(("gx", "gy"), None, None)
    return jax.shard_map(shards, mesh=mesh, in_specs=in_specs, out_specs=out_specs, check_vma=False)
```

profile of v0, /device:TPU:1, one launch (start us, length us, event | category | flops | bytes accessed | tf_op | source)
XLA Modules:
  0.0 125.9 jit_solution(1629589038243137092)
XLA Ops:
  0.0 0.0 copy-start
  0.0 0.5 broadcast.170
  0.5 1.3 %reduce.6 = s32[512]{0:T(512)S(1)} reduce(s32[1,512]{1,0:T(1,128)} %param.14, s32[]{:T(128)} %broadcast.170), dimensions={0}, to_apply=%param.14.reduce_sub_computation.3 | reduce | bytes 4100 | tf_op args[5]
  1.9 0.7 all_to_all.17
  2.6 11.5 %all-to-all-start = ((s32[128,1,4]{2,1,0:T(1,128)}), s32[128,1,4]{2,1,0:T(1,128)S(1)}, u32[]{:S(2)}, u32[]{:S(2)}) async-start(s32[128,1,4]{2,1,0:T(1,128)} %bitcast.6), calls=%async_computation | async-start | bytes 131072 | tf_op jit(solution)/shard_map/all_to_all | solution.py:53
  14.1 0.7 compare_select_fusion.3
  14.8 2.4 %scatter_custom_fusion = s32[512]{0:T(512)S(1)} fusion(s32[512]{0:T(512)S(1)} %bitcast.55, s32[512]{0:T(512)S(1)} %iota.12, s32[]{:T(128)} %constant.32.clone.1), kind=kCustom, calls=%fused_computation.47 | custom fusion | bytes 2052 | tf_op jit(solution)/shard_map/scatter | solution.py:59
  17.2 6.4 %all-to-all-done = s32[128,1,4]{2,1,0:T(1,128)S(1)} async-done(((s32[128,1,4]{2,1,0:T(1,128)}), s32[128,1,4]{2,1,0:T(1,128)S(1)}, u32[]{:S(2)}, u32[]{:S(2)}) %all-to-all-start) | async-done | bytes 2080 | tf_op jit(solution)/shard_map/all_to_all | solution.py:53
  23.7 0.1 reshape.167
  23.8 2.1 %gather_fusion.3 = bf16[512,16,128]{2,1,0:T(8,128)(2,1)S(1)} fusion(bf16[64,16,128]{2,1,0:T(8,128)(2,1)} %param.9, s32[1024]{0:T(1024)S(1)} %pad_clamp_fusion.2), kind=kCustom, calls=%fused_computation.3 | custom fusion | bytes 4196352 | tf_op jit(solution)/shard_map/gather | solution.py:54
  25.9 1.7 %fusion.18 = (bf16[128,1,4,8,128]{4,3,2,1,0:T(8,128)(2,1)}, bf16[128,1,4,8,128]{4,3,2,1,0:T(8,128)(2,1)}) fusion(bf16[128,1,4,16,128]{4,3,2,1,0:T(8,128)(2,1)S(1)} %bitcast.49), kind=kLoop, calls=%fused_computation.50 | loop fusion | bytes 4194304 | tf_op jit(solution)/shard_map/split | solution.py:29
  27.6 0.0 copy-start.1
  27.6 4.5 %all-to-all-start.1 = ((bf16[128,1,4,8,128]{4,3,2,1,0:T(8,128)(2,1)}), bf16[128,1,4,8,128]{4,3,2,1,0:T(8,128)(2,1)S(1)}, u32[]{:S(2)}, u32[]{:S(2)}) async-start(bf16[128,1,4,8,128]{4,3,2,1,0:T(8,128)(2,1)} %get-tuple-element.5), calls=%async_computation.1 | async-start | bytes 2097152 | tf_op jit(solution)/shard_map/all_to_all | solution.py:31
  32.1 0.0 copy-done.1
  32.1 3.3 %gather_fusion.1 = s32[512]{0:T(512)S(1)} fusion(s32[128]{0:T(128)S(1)} %bitcast.45, s32[1024]{0:T(1024)S(1)} %pad_clamp_fusion.3), kind=kCustom, calls=%fused_computation.1 | custom fusion | bytes 6144 | tf_op jit(solution)/shard_map/gather | solution.py:61
  35.5 0.0 copy-start.2
  35.5 0.0 copy-start.5
  35.5 3.5 %gather_fusion.2 = f32[512]{0:T(512)S(1)} fusion(f32[512]{0:T(512)S(1)} %fusion.14, s32[1024]{0:T(1024)S(1)} %pad_clamp_fusion.4), kind=kCustom, calls=%fused_computation.2 | custom fusion | bytes 6144 | tf_op jit(solution)/shard_map/gather | solution.py:62
  39.0 0.0 copy-done
  39.1 3.5 %gather_fusion = s32[512]{0:T(512)S(1)} fusion(s32[512]{0:T(512)S(1)} %bitcast.44, s32[1024]{0:T(1024)S(1)} %pad_clamp_fusion.4), kind=kCustom, calls=%fused_computation | custom fusion | bytes 6144 | tf_op jit(solution)/shard_map/gather | solution.py:63
  42.6 0.0 copy-done.2
  42.6 0.0 copy-done.5
  42.6 0.1 multiply_convert_fusion.1
  42.7 0.2 copy.27
  42.9 2.0 %gather_fusion.5 = bf16[512,16,128]{2,1,0:T(8,128)(2,1)S(1)} fusion(bf16[64,16,128]{2,1,0:T(8,128)(2,1)S(1)} %copy.27, s32[1024]{0:T(1024)S(1)} %pad_clamp_fusion.1), kind=kCustom, calls=%fused_computation.5 | custom fusion | bytes 4196352 | tf_op jit(solution)/shard_map/gather | solution.py:79
  44.9 6.4 %all-to-all-done.1 = bf16[128,1,4,8,128]{4,3,2,1,0:T(8,128)(2,1)S(1)} async-done(((bf16[128,1,4,8,128]{4,3,2,1,0:T(8,128)(2,1)}), bf16[128,1,4,8,128]{4,3,2,1,0:T(8,128)(2,1)S(1)}, u32[]{:S(2)}, u32[]{:S(2)}) %all-to-all-start.1) | async-done | bytes 1048608 | tf_op jit(solution)/shard_map/all_to_all | solution.py:31
  51.3 5.4 %all-to-all-start.2 = ((bf16[128,1,4,8,128]{4,3,2,1,0:T(8,128)(2,1)}), bf16[128,1,4,8,128]{4,3,2,1,0:T(8,128)(2,1)}, u32[]{:S(2)}, u32[]{:S(2)}) async-start(bf16[128,1,4,8,128]{4,3,2,1,0:T(8,128)(2,1)} %get-tuple-element.6), calls=%async_computation.2 | async-start | bytes 2097152 | tf_op jit(solution)/shard_map/all_to_all | solution.py:31
  56.8 9.1 %multiply_convert_fusion = bf16[512,16,128]{2,1,0:T(8,128)(2,1)} fusion(bf16[512,16,128]{2,1,0:T(8,128)(2,1)S(1)} %gather_fusion.5, bf16[512,128,128]{2,1,0:T(8,128)(2,1)} %param.13, f32[512]{0:T(512)S(1)} %gather_fusion.2), kind=kOutput, calls=%fused_computation.9 | convolution fusion | flops 270532608 | bytes 20973568 | tf_op jit(solution)/shard_map/mij,mbi->mbj/dot_general | solution.py:80
  65.9 4.0 %gather_fusion.6 = bf16[512,16,128]{2,1,0:T(8,128)(2,1)} fusion(bf16[512,16,128]{2,1,0:T(8,128)(2,1)} %multiply_convert_fusion, s32[1024]{0:T(1024)S(1)} %pad_clamp_fusion), kind=kCustom, calls=%fused_computation.6 | custom fusion | bytes 4196352 | tf_op jit(solution)/shard_map/gather | solution.py:84
  69.9 5.9 %all-to-all-done.2 = bf16[128,1,4,8,128]{4,3,2,1,0:T(8,128)(2,1)} async-done(((bf16[128,1,4,8,128]{4,3,2,1,0:T(8,128)(2,1)}), bf16[128,1,4,8,128]{4,3,2,1,0:T(8,128)(2,1)}, u32[]{:S(2)}, u32[]{:S(2)}) %all-to-all-start.2) | async-done | bytes 1048608 | tf_op jit(solution)/shard_map/all_to_all | solution.py:31
  75.8 5.5 %all-to-all-start.3 = ((bf16[128,4,16,128]{3,2,1,0:T(8,128)(2,1)}), bf16[128,4,16,128]{3,2,1,0:T(8,128)(2,1)}, u32[]{:S(2)}, u32[]{:S(2)}) async-start(bf16[128,4,16,128]{3,2,1,0:T(8,128)(2,1)} %bitcast.15), calls=%async_computation.3 | async-start | bytes 4194304 | tf_op jit(solution)/shard_map/all_to_all | solution.py:85
  81.3 0.8 reduce.7
  82.0 0.1 eq.34
  82.1 3.0 %pad_maximum_fusion = bf16[128,1,4,16,128]{4,3,2,1,0:T(8,128)(2,1)} fusion(bf16[128,1,4,8,128]{4,3,2,1,0:T(8,128)(2,1)} %all-to-all-done.2, bf16[128,1,4,8,128]{4,3,2,1,0:T(8,128)(2,1)S(1)} %all-to-all-done.1), kind=kLoop, calls=%fused_computation.11 | loop fusion | flops 4194304 | bytes 4194304 | tf_op jit(solution)/shard_map/concatenate | solution.py:32
  85.2 2.8 %gather_fusion.4 = bf16[512,16,128]{2,1,0:T(8,128)(2,1)S(1)} fusion(bf16[512,16,128]{2,1,0:T(8,128)(2,1)} %bitcast.50, s32[1024]{0:T(1024)S(1)} %pad_clamp_fusion.4), kind=kCustom, calls=%fused_computation.4 | custom fusion | bytes 4196352 | tf_op jit(solution)/shard_map/gather | solution.py:64
  88.0 11.7 %fusion.19 = f32[512,16,128]{2,1,0:T(8,128)S(1)} fusion(bf16[512,16,128]{2,1,0:T(8,128)(2,1)S(1)} %gather_fusion.4, bf16[512,128,128]{2,1,0:T(8,128)(2,1)} %param.13), kind=kOutput, calls=%fused_computation.51 | convolution fusion | flops 268435456 | bytes 23068672 | tf_op jit(solution)/shard_map/mij,mbj->mbi/dot_general | solution.py:65
  99.7 4.0 %copy.39 = f32[64,8,16,128]{3,1,2,0:T(8,128)} copy(f32[64,8,16,128]{3,2,1,0:T(8,128)S(1)} %bitcast.46) | data formatting | bytes 8388608
  103.6 5.4 %copy.25 = f32[2048,512]{1,0:T(8,128)} copy(f32[2048,512]{0,1:T(8,128)} %bitcast.48) | data formatting | bytes 8388608 | tf_op jit(solution)/shard_map/dot_general | solution.py:72
  109.0 2.5 %all-to-all-done.3 = bf16[128,4,16,128]{3,2,1,0:T(8,128)(2,1)} async-done(((bf16[128,4,16,128]{3,2,1,0:T(8,128)(2,1)}), bf16[128,4,16,128]{3,2,1,0:T(8,128)(2,1)}, u32[]{:S(2)}, u32[]{:S(2)}) %all-to-all-start.3) | async-done | bytes 2097184 | tf_op jit(solution)/shard_map/all_to_all | solution.py:85
  111.5 2.1 %copy.40 = bf16[64,8,16,128]{3,1,2,0:T(8,128)(2,1)S(1)} copy(bf16[64,8,16,128]{3,2,1,0:T(8,128)(2,1)} %bitcast.23) | data formatting | bytes 4194304
  113.6 2.5 %copy.28 = bf16[512,2048]{0,1:T(8,128)(2,1)} copy(bf16[512,2048]{1,0:T(8,128)(2,1)S(1)} %bitcast.51) | data formatting | bytes 4194304 | tf_op jit(solution)/shard_map/reshape | solution.py:92
  116.2 0.0 copy-start.3
  116.2 0.0 copy-start.4
  116.2 2.4 %convolution_divide_fusion = f32[64,16,128]{2,0,1:T(8,128)S(1)} fusion(bf16[16,128,512]{2,1,0:T(8,128)(2,1)} %bitcast.52, f32[64,128]{1,0:T(8,128)S(1)} %copy-done.5, s32[512]{0:T(512)S(1)} %eq.34), kind=kOutput, calls=%fused_computation.12 | convolution fusion | flops 134381568 | bytes 2656256 | tf_op jit(solution)/shard_map/dot_general | solution.py:96
  118.6 0.0 copy-done.3
  118.6 0.0 copy-done.4
  118.6 6.2 %fusion.1 = f32[64,16,128]{2,0,1:T(8,128)S(1)} fusion(f32[64,16,128]{2,0,1:T(8,128)S(1)} %convolution_divide_fusion, f32[16,128,512]{2,1,0:T(8,128)} %bitcast.47, f32[64,16,128]{2,1,0:T(8,128)S(1)} %copy-done.3, f32[64,16,128]{2,1,0:T(8,128)S(1)} %copy-done.4, f32[512]{0:T(512)S(1)} %gather_fusion.2, s32[512]{0:T(512)S(1)} %gather_fusion), kind=kOutput, calls=%fused_computation.15 | convolution fusion | flops 805765120 | bytes 6295552 | tf_op jit(solution)/shard_map/dot_general | solution.py:72
  124.8 1.1 copy.31
  (11 shorter events, 0.1 us)
Async XLA Ops:
  0.0 39.0 %copy-start = (s32[1,512]{1,0:T(1,128)S(1)}, s32[1,512]{1,0:T(1,128)}, u32[]{:S(2)}) copy-start(s32[1,512]{1,0:T(1,128)} %param.15) | copy-start | bytes 6148
  2.6 21.1 %all-to-all-start = ((s32[128,1,4]{2,1,0:T(1,128)}), s32[128,1,4]{2,1,0:T(1,128)S(1)}, u32[]{:S(2)}, u32[]{:S(2)}) async-start(s32[128,1,4]{2,1,0:T(1,128)} %bitcast.6), calls=%async_computation | async-start | bytes 131072 | tf_op jit(solution)/shard_map/all_to_all | solution.py:53
  27.6 4.5 %copy-start.1 = (s32[1,128]{1,0:T(1,128)S(1)}, s32[1,128]{1,0:T(1,128)}, u32[]{:S(2)}) copy-start(s32[1,128]{1,0:T(1,128)} %param.17) | copy-start | bytes 1540
  27.6 23.7 %all-to-all-start.1 = ((bf16[128,1,4,8,128]{4,3,2,1,0:T(8,128)(2,1)}), bf16[128,1,4,8,128]{4,3,2,1,0:T(8,128)(2,1)S(1)}, u32[]{:S(2)}, u32[]{:S(2)}) async-start(bf16[128,1,4,8,128]{4,3,2,1,0:T(8,128)(2,1)} %get-tuple-element.5), calls=%async_computation.1 | async-start | bytes 2097152 | tf_op jit(solution)/shard_map/all_to_all | solution.py:31
  35.5 7.1 %copy-start.2 = (bf16[64,16,128]{2,1,0:T(8,128)(2,1)S(1)}, bf16[64,16,128]{2,1,0:T(8,128)(2,1)}, u32[]{:S(2)}) copy-start(bf16[64,16,128]{2,1,0:T(8,128)(2,1)} %param.9) | copy-start | bytes 786436
  35.5 7.1 %copy-start.5 = (f32[64,128]{1,0:T(8,128)S(1)}, f32[64,128]{1,0:T(8,128)}, u32[]{:S(2)}) copy-start(f32[64,128]{1,0:T(8,128)} %param.12) | copy-start | bytes 98308
  51.3 24.5 %all-to-all-start.2 = ((bf16[128,1,4,8,128]{4,3,2,1,0:T(8,128)(2,1)}), bf16[128,1,4,8,128]{4,3,2,1,0:T(8,128)(2,1)}, u32[]{:S(2)}, u32[]{:S(2)}) async-start(bf16[128,1,4,8,128]{4,3,2,1,0:T(8,128)(2,1)} %get-tuple-element.6), calls=%async_computation.2 | async-start | bytes 2097152 | tf_op jit(solution)/shard_map/all_to_all | solution.py:31
  75.8 35.7 %all-to-all-start.3 = ((bf16[128,4,16,128]{3,2,1,0:T(8,128)(2,1)}), bf16[128,4,16,128]{3,2,1,0:T(8,128)(2,1)}, u32[]{:S(2)}, u32[]{:S(2)}) async-start(bf16[128,4,16,128]{3,2,1,0:T(8,128)(2,1)} %bitcast.15), calls=%async_computation.3 | async-start | bytes 4194304 | tf_op jit(solution)/shard_map/all_to_all | solution.py:85
  116.2 2.4 %copy-start.3 = (f32[64,16,128]{2,1,0:T(8,128)S(1)}, f32[64,16,128]{2,1,0:T(8,128)}, u32[]{:S(2)}) copy-start(f32[64,16,128]{2,1,0:T(8,128)} %param.10) | copy-start | bytes 1572868
  116.2 2.4 %copy-start.4 = (f32[64,16,128]{2,1,0:T(8,128)S(1)}, f32[64,16,128]{2,1,0:T(8,128)}, u32[]{:S(2)}) copy-start(f32[64,16,128]{2,1,0:T(8,128)} %param.11) | copy-start | bytes 1572868
where the time goes:
time: 127 us; the launch traced here: 126 us
  local copies, waits for them, and re-layouts  42.2 us (33%)
  matrix products  29.5 us (23%)
  starting transfers between devices  26.9 us (21%)
  waiting for transfers between devices  21.2 us (17%)
  other arithmetic  5.93 us (5%)
    all_to_all x2, waiting for transfers between devices, several_exchanges(): lax.all_to_all(piece, axis, split_axis=0, concat_axis=0, tiled=True)  12.3 us
    dot_general x1, matrix products, shards(): jnp.einsum('mij,mbj->mbi', form_factor, rad_stored, preferred_element_typ...  11.7 us
    all_to_all x1, starting transfers between devices, shards(): lax.all_to_all(wanted_rows, ('gx', 'gy'), split_axis=0, concat_axis=0, ti...  11.5 us
    all_to_all x2, starting transfers between devices, several_exchanges(): lax.all_to_all(piece, axis, split_axis=0, concat_axis=0, tiled=True)  9.94 us
    dot_general x1, matrix products, shards(): jnp.einsum('mij,mbi->mbj', form_factor, weighted_stored, preferred_elemen...  9.12 us
    unnamed x15, local copies, waits for them, and re-layouts  6.67 us
    all_to_all x1, waiting for transfers between devices, shards(): lax.all_to_all(wanted_rows, ('gx', 'gy'), split_axis=0, concat_axis=0, ti...  6.4 us
    dot_general x1, matrix products, shards(): jnp.dot(target_table, forward.reshape(link_count, bands * patches), preci...  6.21 us
  transfers between devices with their start and end apart: 4, of which 4 were waited for; matrix products, arithmetic and copies ran while one was open for 45% of the time, Pallas kernels for 0%

commit v1 on v0

v1 whole, which is shorter than its diff:
```python
import functools

import jax
import jax.numpy as jnp
from jax import lax
from jax.experimental import pallas as pl
from jax.experimental.pallas import tpu as pltpu
from jax.sharding import PartitionSpec as P

MESH = pl.DeviceIdType.MESH
DEV = 128
SLOTS = 4
CHUNKS = 8
PER = DEV // CHUNKS
FCH = 8


def position():
    z = lax.axis_index("gx")
    g = lax.axis_index("gy")
    y = lax.div(g, 8)
    x = lax.rem(lax.div(g, 2), 4)
    c = lax.rem(g, 2)
    return z, y, x, c


def peer(me, step, sign):
    z, y, x, c = me
    mixed = lax.rem(step * 37, DEV)
    oc = lax.rem(mixed, 2)
    ox = lax.rem(lax.div(mixed, 2), 4)
    oy = lax.rem(lax.div(mixed, 8), 4)
    oz = lax.div(mixed, 32)
    z2 = lax.rem(z + 4 + sign * oz, 4)
    y2 = lax.rem(y + 4 + sign * oy, 4)
    x2 = lax.rem(x + 4 + sign * ox, 4)
    c2 = lax.rem(c + oc, 2)
    return z2, y2 * 8 + x2 * 2 + c2


def exchange_kernel(
    src_s, tgt_s, blk_s, val_s, rad, area, f_hbm,
    fwd_out, bwd_in, idx_in,
    fv, wtd, sbwd, srad, rrad, sidx, idx_s,
    fsem, isem, idx_send, idx_recv, bwd_send, bwd_recv, rad_send, rad_recv,
):
    me = position()

    def f_copy(i):
        rows = pl.ds(i * (512 // FCH), 512 // FCH)
        return pltpu.make_async_copy(f_hbm.at[rows], fv.at[rows], fsem.at[i])

    for i in range(FCH):
        f_copy(i).start()

    barrier = pltpu.get_barrier_semaphore()

    @pl.loop(1, DEV)
    def _(s):
        pl.semaphore_signal(barrier, inc=1, device_id=peer(me, s, 1), device_id_type=MESH)

    lane = lax.broadcasted_iota(jnp.int32, (1, 128), 1)

    def index_row(s):
        z2, g2 = peer(me, s, 1)
        p = z2 * 32 + g2
        live = val_s[0, p]
        row = jnp.zeros((1, 128), jnp.int32)
        for k in range(SLOTS):
            q = src_s[0, p * SLOTS + k]
            q = jnp.where(k < live, q, q + 64)
            row = jnp.where(lane == k, q, row)
        return row

    idx_in[0] = index_row(0)

    @pl.loop(1, DEV)
    def _(s):
        sidx[s] = index_row(s)

    @pl.loop(0, 64)
    def _(c):
        wtd[c] = (area[pl.ds(c, 1), :] * rad[c].astype(jnp.float32)).astype(jnp.bfloat16)

    pl.semaphore_wait(barrier, DEV - 1)

    def idx_copy(s):
        return pltpu.make_async_remote_copy(
            src_ref=sidx.at[s], dst_ref=idx_in.at[s], send_sem=idx_send, recv_sem=idx_recv,
            device_id=peer(me, s, 1), device_id_type=MESH,
        )

    @pl.loop(1, DEV)
    def _(s):
        idx_copy(s).start()

    for i in range(FCH):
        f_copy(i).wait()

    def bwd_copy(s):
        return pltpu.make_async_remote_copy(
            src_ref=sbwd.at[s], dst_ref=bwd_in.at[s], send_sem=bwd_send,
            recv_sem=bwd_recv, device_id=peer(me, s, 1), device_id_type=MESH,
        )

    def bwd_step(s, out):
        z2, g2 = peer(me, s, 1)
        base = (z2 * 32 + g2) * SLOTS
        for k in range(SLOTS):
            w = wtd[tgt_s[0, base + k]]
            f = fv[blk_s[0, base + k]]
            out[s, k] = jnp.dot(w, f, preferred_element_type=jnp.float32).astype(jnp.bfloat16)

    bwd_step(1, sbwd)

    @pl.loop(2, DEV)
    def _(s):
        bwd_step(s, sbwd)
        bwd_copy(s - 1).start()

    bwd_step(0, bwd_in)
    bwd_copy(DEV - 1).start()

    rest = pl.ds(1, DEV - 1)
    idx_all = pltpu.make_async_remote_copy(
        src_ref=sidx.at[rest], dst_ref=idx_in.at[rest], send_sem=idx_send, recv_sem=idx_recv,
        device_id=peer(me, 1, 1), device_id_type=MESH,
    )
    idx_all.wait()
    to_smem = pltpu.make_async_copy(idx_in, idx_s, isem)
    to_smem.start()
    to_smem.wait()

    def rad_copy(s):
        return pltpu.make_async_remote_copy(
            src_ref=srad.at[s], dst_ref=rrad.at[s], send_sem=rad_send,
            recv_sem=rad_recv.at[lax.div(s, PER)], device_id=peer(me, s, -1), device_id_type=MESH,
        )

    def rad_step(s, out):
        for k in range(SLOTS):
            out[s, k] = rad[lax.rem(idx_s[s, 0, k], 64)]

    rad_step(1, srad)

    @pl.loop(2, DEV)
    def _(s):
        rad_step(s, srad)
        rad_copy(s - 1).start()

    rad_step(0, rrad)
    rad_copy(DEV - 1).start()

    def fwd_step(s):
        z2, g2 = peer(me, s, 1)
        base = (z2 * 32 + g2) * SLOTS
        for k in range(SLOTS):
            f = fv[blk_s[0, base + k]]
            fwd_out[s, k] = lax.dot_general(
                rrad[s, k], f, (((1,), (1,)), ((), ())), preferred_element_type=jnp.float32
            )

    for c in range(CHUNKS):
        first = max(1, c * PER)
        rows = pl.ds(first, (c + 1) * PER - first)
        pltpu.make_async_remote_copy(
            src_ref=srad.at[rows], dst_ref=rrad.at[rows], send_sem=rad_send,
            recv_sem=rad_recv.at[c], device_id=peer(me, 1, -1), device_id_type=MESH,
        ).wait_recv()

        @pl.loop(c * PER, (c + 1) * PER)
        def _(s):
            fwd_step(s)

    bwd_all = pltpu.make_async_remote_copy(
        src_ref=sbwd.at[rest], dst_ref=bwd_in.at[rest], send_sem=bwd_send, recv_sem=bwd_recv,
        device_id=peer(me, 1, 1), device_id_type=MESH,
    )
    bwd_all.wait()
    pltpu.make_async_remote_copy(
        src_ref=srad.at[rest], dst_ref=rrad.at[rest], send_sem=rad_send, recv_sem=rad_recv.at[0],
        device_id=peer(me, 1, -1), device_id_type=MESH,
    ).wait_send()


def combine_kernel(
    tgt_s, val_s, idx_s, fwd, bwd, area, emission, reflectance, out, gat, ret
):
    me = position()
    gat[...] = jnp.zeros_like(gat)
    ret[...] = jnp.zeros_like(ret)

    @pl.loop(0, DEV)
    def _(s):
        z2, g2 = peer(me, s, 1)
        p = z2 * 32 + g2
        live = val_s[0, p]
        for k in range(SLOTS):
            t = jnp.where(k < live, tgt_s[0, p * SLOTS + k], 64)
            q = jnp.minimum(idx_s[s, 0, k], 64)
            gat[t] += fwd[s, k]
            ret[q] += bwd[s, k].astype(jnp.float32)

    @pl.loop(0, 64)
    def _(c):
        irr = gat[c] + ret[c] / area[pl.ds(c, 1), :]
        out[c] = emission[c] + reflectance[c] * irr


def shards(
    radiance, emission, reflectance, patch_area, form_factor,
    source_index, target_index, block_index, valid_count,
):
    smem = pl.BlockSpec(memory_space=pltpu.SMEM)
    vmem = pl.BlockSpec(memory_space=pltpu.VMEM)
    hbm = pl.BlockSpec(memory_space=pl.ANY)
    slab = (DEV, SLOTS, 16, 128)
    dma = pltpu.SemaphoreType.DMA
    fwd, bwd, idx = pl.pallas_call(
        exchange_kernel,
        out_shape=(
            jax.ShapeDtypeStruct(slab, jnp.float32),
            jax.ShapeDtypeStruct(slab, jnp.bfloat16),
            jax.ShapeDtypeStruct((DEV, 1, 128), jnp.int32),
        ),
        in_specs=[smem, smem, smem, smem, vmem, vmem, hbm],
        out_specs=(vmem, vmem, vmem),
        scratch_shapes=[
            pltpu.VMEM((512, 128, 128), jnp.bfloat16),
            pltpu.VMEM((64, 16, 128), jnp.bfloat16),
            pltpu.VMEM(slab, jnp.bfloat16),
            pltpu.VMEM(slab, jnp.bfloat16),
            pltpu.VMEM(slab, jnp.bfloat16),
            pltpu.VMEM((DEV, 1, 128), jnp.int32),
            pltpu.SMEM((DEV, 1, 128), jnp.int32),
            dma((FCH,)), dma, dma, dma, dma, dma, dma, dma((CHUNKS,)),
        ],
        compiler_params=pltpu.CompilerParams(
            collective_id=0, has_side_effects=True, vmem_limit_bytes=48 << 20
        ),
        name="exchange",
    )(source_index, target_index, block_index, valid_count, radiance, patch_area, form_factor)
    return pl.pallas_call(
        combine_kernel,
        out_shape=jax.ShapeDtypeStruct((64, 16, 128), jnp.float32),
        in_specs=[smem, smem, smem, vmem, vmem, vmem, vmem, vmem],
        out_specs=vmem,
        scratch_shapes=[
            pltpu.VMEM((65, 16, 128), jnp.float32),
            pltpu.VMEM((65, 16, 128), jnp.float32),
        ],
        compiler_params=pltpu.CompilerParams(vmem_limit_bytes=24 << 20),
        name="combine",
    )(target_index, valid_count, idx, fwd, bwd, patch_area, emission, reflectance)


def solution(mesh):
    both = ("gx", "gy")
    in_specs = (
        P(both, None, None),
        P(both, None, None),
        P(both, None, None),
        P(both, None),
        P(both, None, None),
        P(both, None),
        P(both, None),
        P(both, None),
        P(both, None),
    )
    return jax.shard_map(
        shards, mesh=mesh, in_specs=in_specs, out_specs=P(both, None, None), check_vma=False
    )
```

time: 127 us -> 99 us (0.78)
  Pallas kernels: 0 us -> 91.6 us
  local copies, waits for them, and re-layouts: 42.2 us -> 6.68 us
  matrix products: 29.5 us -> 0 us
  starting transfers between devices: 26.9 us -> 0 us
  waiting for transfers between devices: 21.2 us -> 0 us
  other arithmetic: 5.93 us -> 0 us
    pallas_call x0 -> x2, Pallas kernels: none -> 91.6 us  [the longest x1 83 us: shards(): pl.pallas_call(exchange_kernel, out_shape=(jax.ShapeDtypeStruct(slab, jnp...]
    dot_general x4 -> x0, matrix products: 29.5 us -> none  [the longest x1 11.7 us: shards(): jnp.einsum('mij,mbj->mbi', form_factor, rad_stored, preferred_element_typ...]
    all_to_all x4 -> x0, starting transfers between devices: 26.9 us -> none  [the longest x1 11.5 us: shards(): lax.all_to_all(wanted_rows, ('gx', 'gy'), split_axis=0, concat_axis=0, ti...]
    gather x7 -> x0, local copies, waits for them, and re-layouts: 21.3 us -> none  [the longest x1 3.99 us: shards(): backward_links = backward[block_row]]
    all_to_all x4 -> x0, waiting for transfers between devices: 21.2 us -> none  [the longest x2 12.3 us: several_exchanges(): lax.all_to_all(piece, axis, split_axis=0, concat_axis=0, tiled=True)]
    dot_general x1 -> x0, local copies, waits for them, and re-layouts: 5.35 us -> none  [shards(): jnp.dot(target_table, forward.reshape(link_count, bands * patches), preci...]
    concatenate x1 -> x0, other arithmetic: 3.03 us -> none  [several_exchanges(): return in_order(jnp.concatenate(outs, axis=cut), concat_dim)]
    reshape x1 -> x0, local copies, waits for them, and re-layouts: 2.51 us -> none  [shards(): arrived = arrived.reshape(link_count, bands * patches).astype(jnp.float32)]
  transfers between devices with their start and end apart: 4 -> 0, of which waited for: 4 -> 0; matrix products, arithmetic and copies ran while one was open for 45% -> 0% of each run, Pallas kernels for 0% -> 0%
where the time goes in v1:
time: 99 us; the launch traced here: 98.4 us
  Pallas kernels  91.6 us (93%)
  local copies, waits for them, and re-layouts  6.68 us (7%)
    pallas_call x1, Pallas kernels, shards(): pl.pallas_call(exchange_kernel, out_shape=(jax.ShapeDtypeStruct(slab, jnp...  83 us
    pallas_call x1, Pallas kernels, shards(): pl.pallas_call(combine_kernel, out_shape=jax.ShapeDtypeStruct((64, 16, 12...  8.68 us
    unnamed x18, local copies, waits for them, and re-layouts  6.68 us

profile of v1, /device:TPU:1, one launch (start us, length us, event | category | flops | bytes accessed | tf_op | source)
XLA Modules:
  0.0 98.4 jit_solution(10449728889534233021)
XLA Ops:
  0.0 0.0 copy-start.2
  0.0 0.0 copy-start.1
  0.0 0.0 copy-start.3
  0.0 1.0 %copy-done.3 = bf16[64,16,128]{2,1,0:T(8,128)(2,1)S(1)} copy-done((bf16[64,16,128]{2,1,0:T(8,128)(2,1)S(1)}, bf16[64,16,128]{2,1,0:T(8,128)(2,1)}, u32[]{:S(2)}) %copy-start.3) | copy-done | bytes 262168
  1.0 0.0 copy-start.4
  1.0 0.8 copy-done.4
  1.8 0.0 copy-start.5
  1.8 0.7 copy-done.5
  2.5 0.0 copy-start.6
  2.5 0.7 copy-done.6
  3.2 0.0 copy-start.7
  3.2 0.7 copy-done.7
  3.8 0.0 copy-start.8
  3.9 0.7 copy-done.8
  4.5 83.0 %exchange.1 = (f32[128,4,16,128]{3,2,1,0:T(8,128)}, bf16[128,4,16,128]{3,2,1,0:T(8,128)(2,1)S(1)}, s32[128,1,128]{2,1,0:T(1,128)S(1)}) custom-call(s32[1,512]{1,0:T(1,128)S(1)} %copy-done.6, s32[1,512]{1,0:T(1,128)S(1)} %copy-done.5, s32[1,512]{1,0:T(1,128)S(1)} %copy-done.7, s32[1,128]{1,0:T(1,128)S(1)} %copy-done.8, bf16[64,16,128]{2,1,0:T(8,128)(2,1)S(1)} %copy-done.3, ...), custom_call_target="tpu_custom_call" | custom-call | tf_op jit(solution)/shard_map/exchange/pallas_call | solution.py:219
  87.5 0.0 copy-done.2
  87.5 0.0 copy-done.1
  87.5 0.0 copy-start
  87.5 2.2 %copy-done = f32[128,4,16,128]{3,2,1,0:T(8,128)S(1)} copy-done((f32[128,4,16,128]{3,2,1,0:T(8,128)S(1)}, f32[128,4,16,128]{3,2,1,0:T(8,128)}, u32[]{:S(2)}) %copy-start) | copy-done | bytes 4194328
  89.7 8.7 %combine.1 = f32[64,16,128]{2,1,0:T(8,128)} custom-call(s32[1,512]{1,0:T(1,128)S(1)} %copy-done.5, s32[1,128]{1,0:T(1,128)S(1)} %copy-done.8, s32[128,1,128]{2,1,0:T(1,128)S(1)} %get-tuple-element.8.idx_s, f32[128,4,16,128]{3,2,1,0:T(8,128)S(1)} %copy-done, bf16[128,4,16,128]{3,2,1,0:T(8,128)(2,1)S(1)} %get-tuple-element.10.bwd, f32[64,128]{1,0:T(8,128)S(1)} %copy-done.4, ...), custom_call_target="tpu_custom_call" | custom-call | tf_op jit(solution)/shard_map/combine/pallas_call | solution.py:243
Async XLA Ops:
  0.0 87.5 %copy-start.2 = (f32[64,16,128]{2,1,0:T(8,128)S(1)}, f32[64,16,128]{2,1,0:T(8,128)}, u32[]{:S(2)}) copy-start(f32[64,16,128]{2,1,0:T(8,128)} %reflectance.1) | copy-start | bytes 1572868
  0.0 87.5 %copy-start.1 = (f32[64,16,128]{2,1,0:T(8,128)S(1)}, f32[64,16,128]{2,1,0:T(8,128)}, u32[]{:S(2)}) copy-start(f32[64,16,128]{2,1,0:T(8,128)} %emission.1) | copy-start | bytes 1572868
  0.0 1.0 %copy-start.3 = (bf16[64,16,128]{2,1,0:T(8,128)(2,1)S(1)}, bf16[64,16,128]{2,1,0:T(8,128)(2,1)}, u32[]{:S(2)}) copy-start(bf16[64,16,128]{2,1,0:T(8,128)(2,1)} %rad.1) | copy-start | bytes 786436
  1.0 0.8 copy-start.4
  1.8 0.7 copy-start.5
  2.5 0.7 copy-start.6
  3.2 0.7 copy-start.7
  3.8 0.7 copy-start.8
  87.5 2.2 %copy-start = (f32[128,4,16,128]{3,2,1,0:T(8,128)S(1)}, f32[128,4,16,128]{3,2,1,0:T(8,128)}, u32[]{:S(2)}) copy-start(f32[128,4,16,128]{3,2,1,0:T(8,128)} %get-tuple-element.9.fwd) | copy-start | bytes 12582916

commit v2 on v1

v2 whole, which is shorter than its diff:
```python
import jax
import jax.numpy as jnp
from jax import lax
from jax.experimental import pallas as pl
from jax.experimental.pallas import tpu as pltpu
from jax.sharding import PartitionSpec as P

MESH = pl.DeviceIdType.MESH
DEV = 128
SLOTS = 4
GROUPS = 32
GRP = DEV // GROUPS
EARLY = 8
CHUNKS = 4
PER = DEV // CHUNKS
FCH = 8
MIX = 59


def position():
    z = lax.axis_index("gx")
    g = lax.axis_index("gy")
    y = lax.div(g, 8)
    x = lax.rem(lax.div(g, 2), 4)
    c = lax.rem(g, 2)
    return z, y, x, c


def peer(me, step, sign):
    z, y, x, c = me
    mixed = lax.rem(step * MIX, DEV)
    oc = lax.rem(mixed, 2)
    ox = lax.rem(lax.div(mixed, 2), 4)
    oy = lax.rem(lax.div(mixed, 8), 4)
    oz = lax.div(mixed, 32)
    z2 = lax.rem(z + 4 + sign * oz, 4)
    y2 = lax.rem(y + 4 + sign * oy, 4)
    x2 = lax.rem(x + 4 + sign * ox, 4)
    c2 = lax.rem(c + oc, 2)
    return z2, y2 * 8 + x2 * 2 + c2


def exchange_kernel(
    src_h, tgt_h, blk_h, val_h, rad_h, area_h, f_h,
    irr,
    src_s, tgt_s, blk_s, val_s, rad, area,
    fv, wtd, sbwd, bwd_0, bwd_1, bwd_2, bwd_3, srad, rrad, fwd, sidx, idx_in, tidx, seq, gat, ret,
    meta_v, idx_s, meta_s,
    lsem, fsem, msem, idx_send, idx_recv, bwd_send, bwd_recv, rad_send, rad_recv,
):
    me = position()
    bwd_in = (bwd_0, bwd_1, bwd_2, bwd_3)

    loads = [
        pltpu.make_async_copy(a, b, lsem.at[i])
        for i, (a, b) in enumerate(
            [(src_h, src_s), (tgt_h, tgt_s), (blk_h, blk_s), (val_h, val_s), (rad_h, rad), (area_h, area)]
        )
    ]
    for load in loads:
        load.start()

    def f_copy(i):
        rows = pl.ds(i * (512 // FCH), 512 // FCH)
        return pltpu.make_async_copy(f_h.at[rows], fv.at[rows], fsem.at[i])

    for i in range(FCH):
        f_copy(i).start()

    barrier = pltpu.get_barrier_semaphore()

    @pl.loop(1, DEV)
    def _(s):
        pl.semaphore_signal(barrier, inc=1, device_id=peer(me, s, 1), device_id_type=MESH)

    for load in loads:
        load.wait()

    lane = lax.broadcasted_iota(jnp.int32, (1, 128), 1)

    @pl.loop(0, DEV)
    def _(s):
        z2, g2 = peer(me, s, 1)
        p = z2 * 32 + g2
        live = val_s[0, p]
        srow = jnp.zeros((1, 128), jnp.int32)
        trow = jnp.zeros((1, 128), jnp.int32)
        for k in range(SLOTS):
            dead = jnp.where(k < live, 0, 64)
            srow = jnp.where(lane == k, src_s[0, p * SLOTS + k] + dead, srow)
            trow = jnp.where(lane == k, tgt_s[0, p * SLOTS + k] + dead, trow)
        sidx[s] = srow
        tidx[s] = trow

    idx_in[0] = sidx[0]

    @pl.loop(0, 64)
    def _(c):
        wtd[c] = (area[pl.ds(c, 1), :] * rad[c].astype(jnp.float32)).astype(jnp.bfloat16)

    pl.semaphore_wait(barrier, DEV - 1)

    def idx_copy(rows, s):
        return pltpu.make_async_remote_copy(
            src_ref=sidx.at[rows], dst_ref=idx_in.at[rows], send_sem=idx_send, recv_sem=idx_recv,
            device_id=peer(me, s, 1), device_id_type=MESH,
        )

    @pl.loop(1, DEV)
    def _(s):
        idx_copy(s, s).start()

    def bwd_copy(first, count, s, c):
        return pltpu.make_async_remote_copy(
            src_ref=sbwd.at[pl.ds(first, count)],
            dst_ref=bwd_in[c].at[pl.ds(first - c * PER, count)],
            send_sem=bwd_send.at[c], recv_sem=bwd_recv.at[c],
            device_id=peer(me, s, 1), device_id_type=MESH,
        )

    def bwd_rest(c):
        first = max(1, c * PER)
        return bwd_copy(first, (c + 1) * PER - first, 1, c)

    def rad_copy(rows, s, c):
        return pltpu.make_async_remote_copy(
            src_ref=srad.at[rows], dst_ref=rrad.at[rows], send_sem=rad_send,
            recv_sem=rad_recv.at[c], device_id=peer(me, s, -1), device_id_type=MESH,
        )

    def send_rad(g, first=0):
        for j in range(first, GRP):
            s = g * GRP + j
            rad_copy(s, s, lax.div(s, PER)).start()

    def send_bwd(g, c, first=0):
        for j in range(first, GRP):
            s = g * GRP + j
            bwd_copy(s, 1, s, c).start()

    def bwd_group(g):
        for j in range(GRP):
            s = g * GRP + j
            z2, g2 = peer(me, s, 1)
            base = (z2 * 32 + g2) * SLOTS
            for k in range(0, SLOTS, 2):
                w = jnp.concatenate([wtd[tgt_s[0, base + k]], wtd[tgt_s[0, base + k + 1]]], axis=0)
                f = jnp.concatenate([fv[blk_s[0, base + k]], fv[blk_s[0, base + k + 1]]], axis=1)
                r = jnp.dot(w, f, preferred_element_type=jnp.float32)
                sbwd[s, k] = r[:16, :128].astype(jnp.bfloat16)
                sbwd[s, k + 1] = r[16:, 128:].astype(jnp.bfloat16)

    def fwd_group(g):
        for j in range(GRP):
            s = g * GRP + j
            z2, g2 = peer(me, s, 1)
            base = (z2 * 32 + g2) * SLOTS
            for k in range(0, SLOTS, 2):
                v = jnp.concatenate([rrad[s, k], rrad[s, k + 1]], axis=0)
                f = jnp.concatenate([fv[blk_s[0, base + k]], fv[blk_s[0, base + k + 1]]], axis=0)
                r = lax.dot_general(v, f, (((1,), (1,)), ((), ())), preferred_element_type=jnp.float32)
                fwd[s, k] = r[:16, :128]
                fwd[s, k + 1] = r[16:, 128:]

    for i in range(FCH):
        f_copy(i).wait()

    bwd_group(0)
    bwd_group(1)
    send_bwd(0, 0, 1)

    @pl.loop(2, EARLY + 1)
    def _(g):
        bwd_group(g)
        send_bwd(g - 1, 0)

    @pl.loop(EARLY + 1, GROUPS)
    def _(g):
        bwd_group(g)

    for k in range(SLOTS):
        bwd_0[0, k] = sbwd[0, k]

    rest = pl.ds(1, DEV - 1)
    idx_copy(rest, 1).wait()
    to_smem = pltpu.make_async_copy(idx_in, idx_s, msem.at[0])
    to_smem.start()
    to_smem.wait()

    def rad_group(g):
        for j in range(GRP):
            s = g * GRP + j
            for k in range(SLOTS):
                srad[s, k] = rad[lax.rem(idx_s[s, 0, k], 64)]

    rad_group(0)
    rad_group(1)
    send_rad(0, 1)

    @pl.loop(2, GROUPS)
    def _(g):
        rad_group(g)
        send_rad(g - 1)

    for k in range(SLOTS):
        rrad[0, k] = srad[0, k]
    send_rad(GROUPS - 1)

    for c in range(EARLY // (GROUPS // CHUNKS), CHUNKS):

        @pl.loop(c * (GROUPS // CHUNKS), (c + 1) * (GROUPS // CHUNKS))
        def _(g):
            send_bwd(g, c)

    def order(ids, c, base):
        block = ids[pl.ds(c * PER, PER)].reshape(PER, 128)
        q = jnp.concatenate(
            [jnp.broadcast_to(block[:, k : k + 1], (PER, 128)) for k in range(SLOTS)], axis=0
        )
        lanes = lax.broadcasted_iota(jnp.int32, (128, 128), 1)
        key = q * 128 + lax.broadcasted_iota(jnp.int32, (128, 128), 0)
        rank = jnp.sum((key.T < key).astype(jnp.int32), axis=1, keepdims=True)
        meta_v[base + 2 * c] = jnp.sum(jnp.where(rank == lanes, key, 0), axis=0, keepdims=True)
        upto = jnp.sum((q <= lanes).astype(jnp.int32), axis=0, keepdims=True)
        below = jnp.sum((q < lanes).astype(jnp.int32), axis=0, keepdims=True)
        meta_v[base + 2 * c + 1] = jnp.where(upto > below, upto, 0)

    @pl.loop(0, CHUNKS)
    def _(c):
        order(tidx, c, 0)
        order(idx_in, c, 2 * CHUNKS)

    to_smem = pltpu.make_async_copy(meta_v, meta_s, msem.at[1])
    to_smem.start()
    to_smem.wait()

    seq[0] = jnp.zeros((16, 128), jnp.float32)
    gat[...] = jnp.zeros_like(gat)
    ret[...] = jnp.zeros_like(ret)

    def scan(values, offset, total, c, base):
        def body(i, carry):
            acc, last = carry
            for j in range(8):
                n = i * 8 + j
                key = meta_s[base + 2 * c, 0, n]
                q = lax.div(key, 128)
                item = lax.rem(key, 128)
                x = values[offset + lax.rem(item, PER), lax.div(item, PER)].astype(jnp.float32)
                acc = acc * jnp.where(q == last, 1.0, 0.0) + x
                seq[n + 1] = acc
                last = q
            return acc, last

        lax.fori_loop(0, 16, body, (jnp.zeros((16, 128), jnp.float32), jnp.int32(-1)))

        @pl.loop(0, 16)
        def _(i):
            for j in range(4):
                t = i * 4 + j
                total[t] += seq[meta_s[base + 2 * c + 1, 0, t]]

    for c in range(CHUNKS):
        first = max(1, c * PER)
        rad_copy(pl.ds(first, (c + 1) * PER - first), 1, c).wait_recv()

        @pl.loop(c * (GROUPS // CHUNKS), (c + 1) * (GROUPS // CHUNKS))
        def _(g):
            fwd_group(g)

        scan(fwd, c * PER, gat, c, 0)

    for c in range(CHUNKS):
        bwd_rest(c).wait_recv()
        scan(bwd_in[c], 0, ret, c, 2 * CHUNKS)

    @pl.loop(0, 64)
    def _(c):
        irr[c] = gat[c] + ret[c] / area[pl.ds(c, 1), :]

    for c in range(CHUNKS):
        bwd_rest(c).wait_send()
    rad_copy(rest, 1, 0).wait_send()


def shards(
    radiance, emission, reflectance, patch_area, form_factor,
    source_index, target_index, block_index, valid_count,
):
    hbm = pl.BlockSpec(memory_space=pltpu.HBM)
    vmem = pl.BlockSpec(memory_space=pltpu.VMEM)
    slab = (DEV, SLOTS, 16, 128)
    rows = (DEV, 1, 128)
    dma = pltpu.SemaphoreType.DMA
    irr = pl.pallas_call(
        exchange_kernel,
        out_shape=jax.ShapeDtypeStruct((64, 16, 128), jnp.float32),
        in_specs=[hbm] * 7,
        out_specs=vmem,
        scratch_shapes=[
            pltpu.SMEM((1, 512), jnp.int32),
            pltpu.SMEM((1, 512), jnp.int32),
            pltpu.SMEM((1, 512), jnp.int32),
            pltpu.SMEM((1, 128), jnp.int32),
            pltpu.VMEM((64, 16, 128), jnp.bfloat16),
            pltpu.VMEM((64, 128), jnp.float32),
            pltpu.VMEM((512, 128, 128), jnp.bfloat16),
            pltpu.VMEM((64, 16, 128), jnp.bfloat16),
            pltpu.VMEM(slab, jnp.bfloat16),
            *[pltpu.VMEM((PER, SLOTS, 16, 128), jnp.bfloat16) for _ in range(CHUNKS)],
            pltpu.VMEM(slab, jnp.bfloat16),
            pltpu.VMEM(slab, jnp.bfloat16),
            pltpu.VMEM(slab, jnp.float32),
            pltpu.VMEM(rows, jnp.int32),
            pltpu.VMEM(rows, jnp.int32),
            pltpu.VMEM(rows, jnp.int32),
            pltpu.VMEM((136, 16, 128), jnp.float32),
            pltpu.VMEM((64, 16, 128), jnp.float32),
            pltpu.VMEM((64, 16, 128), jnp.float32),
            pltpu.VMEM((4 * CHUNKS, 1, 128), jnp.int32),
            pltpu.SMEM(rows, jnp.int32),
            pltpu.SMEM((4 * CHUNKS, 1, 128), jnp.int32),
            dma((6,)), dma((FCH,)), dma((2,)), dma, dma, dma((CHUNKS,)), dma((CHUNKS,)), dma, dma((CHUNKS,)),
        ],
        compiler_params=pltpu.CompilerParams(
            collective_id=0, has_side_effects=True, vmem_limit_bytes=67043328
        ),
        name="exchange",
    )(
        source_index, target_index, block_index, valid_count, radiance, patch_area, form_factor
    )
    return emission + reflectance * irr


def solution(mesh):
    both = ("gx", "gy")
    in_specs = (
        P(both, None, None),
        P(both, None, None),
        P(both, None, None),
        P(both, None),
        P(both, None, None),
        P(both, None),
        P(both, None),
        P(both, None),
        P(both, None),
    )
    return jax.shard_map(
        shards, mesh=mesh, in_specs=in_specs, out_specs=P(both, None, None), check_vma=False
    )
```

time: 99 us -> 88.1 us (0.89)
  the two profiles are of different devices: /device:TPU:1 before, /device:TPU:22 now
where the time goes in v2:
time: 88.1 us; the launch traced here: 87.9 us
  Pallas kernels  85.5 us (97%)
  other arithmetic  2.38 us (3%)
    pallas_call x1, Pallas kernels, shards(): pl.pallas_call(exchange_kernel, out_shape=jax.ShapeDtypeStruct((64, 16, 1...  85.5 us
    add x1, other arithmetic, shards(): return emission + reflectance * irr  2.38 us

profile of v2, /device:TPU:22, one launch (start us, length us, event | category | flops | bytes accessed | tf_op | source)
XLA Modules:
  0.0 87.9 jit_solution(8247029500723678478)
XLA Ops:
  0.0 85.5 %exchange.1 = f32[64,16,128]{2,1,0:T(8,128)} custom-call(s32[1,512]{1,0:T(1,128)} %src_h.1, s32[1,512]{1,0:T(1,128)} %tgt_h.1, s32[1,512]{1,0:T(1,128)} %blk_h.1, s32[1,128]{1,0:T(1,128)} %val_h.1, bf16[64,16,128]{2,1,0:T(8,128)(2,1)} %rad_h.1, f32[64,128]{1,0:T(8,128)} %area_h.1, bf16[512,128,128]{2,1,0:T(8,128)(2,1)} %f_h.1), custom_call_target="tpu_custom_call" | custom-call | tf_op jit(solution)/shard_map/exchange/pallas_call | solution.py:295
  85.5 2.4 %multiply_add_fusion = f32[64,16,128]{2,1,0:T(8,128)} fusion(f32[64,16,128]{2,1,0:T(8,128)} %param.10, f32[64,16,128]{2,1,0:T(8,128)} %param.11, f32[64,16,128]{2,1,0:T(8,128)} %exchange.1), kind=kLoop, calls=%fused_computation | loop fusion | flops 262144 | bytes 2097152 | tf_op jit(solution)/shard_map/add | solution.py:332

commit v3 on v2

--- a/solution.py
+++ b/solution.py
@@ -10,11 +10,11 @@
 SLOTS = 4
 GROUPS = 32
 GRP = DEV // GROUPS
-EARLY = 8
+EARLY = 2
 CHUNKS = 4
 PER = DEV // CHUNKS
 FCH = 8
-MIX = 59
+MIX = 37
 
 
 def position():
@@ -69,34 +69,39 @@
 
     barrier = pltpu.get_barrier_semaphore()
 
-    @pl.loop(1, DEV)
-    def _(s):
-        pl.semaphore_signal(barrier, inc=1, device_id=peer(me, s, 1), device_id_type=MESH)
+    def by_peer(step):
+        for s in range(1, GRP):
+            step(s)
+
+        @pl.loop(1, GROUPS)
+        def _(g):
+            for j in range(GRP):
+                step(g * GRP + j)
+
+    by_peer(
+        lambda s: pl.semaphore_signal(barrier, inc=1, device_id=peer(me, s, 1), device_id_type=MESH)
+    )
 
     for load in loads:
         load.wait()
 
     lane = lax.broadcasted_iota(jnp.int32, (1, 128), 1)
 
-    @pl.loop(0, DEV)
-    def _(s):
-        z2, g2 = peer(me, s, 1)
-        p = z2 * 32 + g2
-        live = val_s[0, p]
-        srow = jnp.zeros((1, 128), jnp.int32)
-        trow = jnp.zeros((1, 128), jnp.int32)
-        for k in range(SLOTS):
-            dead = jnp.where(k < live, 0, 64)
-            srow = jnp.where(lane == k, src_s[0, p * SLOTS + k] + dead, srow)
-            trow = jnp.where(lane == k, tgt_s[0, p * SLOTS + k] + dead, trow)
-        sidx[s] = srow
-        tidx[s] = trow
-
+    def fill(rows, table):
+        @pl.loop(0, GROUPS)
+        def _(g):
+            for j in range(GRP):
+                s = g * GRP + j
+                z2, g2 = peer(me, s, 1)
+                p = z2 * 32 + g2
+                live = val_s[0, p]
+                row = jnp.zeros((1, 128), jnp.int32)
+                for k in range(SLOTS):
+                    row = jnp.where(lane == k, table[0, p * SLOTS + k] + jnp.where(k < live, 0, 64), row)
+                rows[s] = row
+
+    fill(sidx, src_s)
     idx_in[0] = sidx[0]
-
-    @pl.loop(0, 64)
-    def _(c):
-        wtd[c] = (area[pl.ds(c, 1), :] * rad[c].astype(jnp.float32)).astype(jnp.bfloat16)
 
     pl.semaphore_wait(barrier, DEV - 1)
 
@@ -106,9 +111,13 @@
             device_id=peer(me, s, 1), device_id_type=MESH,
         )
 
-    @pl.loop(1, DEV)
-    def _(s):
-        idx_copy(s, s).start()
+    by_peer(lambda s: idx_copy(s, s).start())
+
+    @pl.loop(0, 16)
+    def _(i):
+        for j in range(4):
+            c = i * 4 + j
+            wtd[c] = (area[pl.ds(c, 1), :] * rad[c].astype(jnp.float32)).astype(jnp.bfloat16)
 
     def bwd_copy(first, count, s, c):
         return pltpu.make_async_remote_copy(
@@ -169,14 +178,25 @@
     bwd_group(1)
     send_bwd(0, 0, 1)
 
-    @pl.loop(2, EARLY + 1)
+    lap = GROUPS // CHUNKS
+
+    @pl.loop(2, lap + 1)
     def _(g):
         bwd_group(g)
         send_bwd(g - 1, 0)
 
-    @pl.loop(EARLY + 1, GROUPS)
+    for c in range(1, EARLY):
+
+        @pl.loop(c * lap + 1, (c + 1) * lap + 1)
+        def _(g):
+            bwd_group(g)
+            send_bwd(g - 1, c)
+
+    @pl.loop(EARLY * lap + 1, GROUPS)
     def _(g):
         bwd_group(g)
+
+    fill(tidx, tgt_s)
 
     for k in range(SLOTS):
         bwd_0[0, k] = sbwd[0, k]
@@ -206,9 +226,9 @@
         rrad[0, k] = srad[0, k]
     send_rad(GROUPS - 1)
 
-    for c in range(EARLY // (GROUPS // CHUNKS), CHUNKS):
-
-        @pl.loop(c * (GROUPS // CHUNKS), (c + 1) * (GROUPS // CHUNKS))
+    for c in range(EARLY, CHUNKS):
+
+        @pl.loop(c * lap, (c + 1) * lap)
         def _(g):
             send_bwd(g, c)
 
@@ -264,7 +284,7 @@
         first = max(1, c * PER)
         rad_copy(pl.ds(first, (c + 1) * PER - first), 1, c).wait_recv()
 
-        @pl.loop(c * (GROUPS // CHUNKS), (c + 1) * (GROUPS // CHUNKS))
+        @pl.loop(c * lap, (c + 1) * lap)
         def _(g):
             fwd_group(g)
 
@@ -323,11 +343,11 @@
             dma((6,)), dma((FCH,)), dma((2,)), dma, dma, dma((CHUNKS,)), dma((CHUNKS,)), dma, dma((CHUNKS,)),
         ],
         compiler_params=pltpu.CompilerParams(
-            collective_id=0, has_side_effects=True, vmem_limit_bytes=67043328
+            collective_id=0, has_side_effects=True, vmem_limit_bytes=48 << 20
         ),
         name="exchange",
     )(
-        source_index, target_index, block_index, valid_count, radiance, patch_area, form_factor
+        *[pltpu.with_memory_space_constraint(v, pltpu.HBM) for v in (source_index, target_index, block_index, valid_count, radiance, patch_area, form_factor)]
     )
     return emission + reflectance * irr
 

time: 88.1 us -> 72.7 us (0.83)
  the two profiles are of different devices: /device:TPU:22 before, /device:TPU:1 now
where the time goes in v3:
time: 72.7 us; the launch traced here: 71.6 us
  Pallas kernels  70.6 us (97%)
  other arithmetic  0.89 us (1%)
    pallas_call x1, Pallas kernels, shards(): pl.pallas_call(exchange_kernel, out_shape=jax.ShapeDtypeStruct((64, 16, 1...  70.6 us

profile of v3, /device:TPU:1, one launch (start us, length us, event | category | flops | bytes accessed | tf_op | source)
XLA Modules:
  0.0 71.6 jit_solution(17583112177615172283)
XLA Ops:
  0.0 0.0 copy-start.1
  0.0 0.0 copy-start
  0.0 70.6 %exchange.1 = f32[64,16,128]{2,1,0:T(8,128)S(1)} custom-call(s32[1,512]{1,0:T(1,128)} %src_h.1, s32[1,512]{1,0:T(1,128)} %tgt_h.1, s32[1,512]{1,0:T(1,128)} %blk_h.1, s32[1,128]{1,0:T(1,128)} %val_h.1, bf16[64,16,128]{2,1,0:T(8,128)(2,1)} %rad_h.1, f32[64,128]{1,0:T(8,128)} %area_h.1, bf16[512,128,128]{2,1,0:T(8,128)(2,1)} %f_h.1), custom_call_target="tpu_custom_call" | custom-call | tf_op jit(solution)/shard_map/exchange/pallas_call | solution.py:315
  70.6 0.0 copy-done.1
  70.7 0.0 copy-done
  70.7 0.9 %multiply_add_fusion = f32[64,16,128]{2,1,0:T(8,128)} fusion(f32[64,16,128]{2,1,0:T(8,128)S(1)} %copy-done, f32[64,16,128]{2,1,0:T(8,128)S(1)} %copy-done.1, f32[64,16,128]{2,1,0:T(8,128)S(1)} %exchange.1), kind=kLoop, calls=%fused_computation | loop fusion | flops 262144 | bytes 2097152 | tf_op jit(solution)/shard_map/add | solution.py:352
Async XLA Ops:
  0.0 70.6 %copy-start.1 = (f32[64,16,128]{2,1,0:T(8,128)S(1)}, f32[64,16,128]{2,1,0:T(8,128)}, u32[]{:S(2)}) copy-start(f32[64,16,128]{2,1,0:T(8,128)} %param.11) | copy-start | bytes 1572868
  0.0 70.7 %copy-start = (f32[64,16,128]{2,1,0:T(8,128)S(1)}, f32[64,16,128]{2,1,0:T(8,128)}, u32[]{:S(2)}) copy-start(f32[64,16,128]{2,1,0:T(8,128)} %param.10) | copy-start | bytes 1572868

commit v4 on v3

--- a/solution.py
+++ b/solution.py
@@ -14,7 +14,7 @@
 CHUNKS = 4
 PER = DEV // CHUNKS
 FCH = 8
-MIX = 37
+MIX = 13
 
 
 def position():
@@ -40,13 +40,26 @@
     return z2, y2 * 8 + x2 * 2 + c2
 
 
+def index_spot(step):
+    mixed = lax.rem(step * MIX, DEV)
+    return lax.rem(mixed, 2), lax.div(mixed, 2)
+
+
+def chip(me, m):
+    z, y, x, _ = me
+    return (
+        lax.rem(z + lax.div(m, 16), 4),
+        lax.rem(y + lax.rem(lax.div(m, 4), 4), 4) * 8 + lax.rem(x + lax.rem(m, 4), 4) * 2,
+    )
+
+
 def exchange_kernel(
     src_h, tgt_h, blk_h, val_h, rad_h, area_h, f_h,
     irr,
     src_s, tgt_s, blk_s, val_s, rad, area,
-    fv, wtd, sbwd, bwd_0, bwd_1, bwd_2, bwd_3, srad, rrad, fwd, sidx, idx_in, tidx, seq, gat, ret,
-    meta_v, idx_s, meta_s,
-    lsem, fsem, msem, idx_send, idx_recv, bwd_send, bwd_recv, rad_send, rad_recv,
+    fv, wtd, sbwd, bwd_0, bwd_1, bwd_2, bwd_3, srad, rrad, fwd, sidx, idx_in, tidx, ridx, seq, gat, ret,
+    meta_v, meta_s,
+    lsem, fsem, msem, idx_send, idx_recv, pair_send, pair_recv, bwd_send, bwd_recv, rad_send, rad_recv,
 ):
     me = position()
     bwd_in = (bwd_0, bwd_1, bwd_2, bwd_3)
@@ -100,24 +113,56 @@
                     row = jnp.where(lane == k, table[0, p * SLOTS + k] + jnp.where(k < live, 0, 64), row)
                 rows[s] = row
 
-    fill(sidx, src_s)
-    idx_in[0] = sidx[0]
-
-    pl.semaphore_wait(barrier, DEV - 1)
-
-    def idx_copy(rows, s):
-        return pltpu.make_async_remote_copy(
-            src_ref=sidx.at[rows], dst_ref=idx_in.at[rows], send_sem=idx_send, recv_sem=idx_recv,
-            device_id=peer(me, s, 1), device_id_type=MESH,
-        )
-
-    by_peer(lambda s: idx_copy(s, s).start())
+    @pl.loop(0, 32)
+    def _(i):
+        for j in range(2):
+            m = i * 2 + j
+            z2, g2 = chip(me, m)
+            row = jnp.zeros((1, 128), jnp.int32)
+            for c in range(2):
+                p = z2 * 32 + g2 + c
+                live = val_s[0, p]
+                for k in range(SLOTS):
+                    q = src_s[0, p * SLOTS + k] + jnp.where(k < live, 0, 64)
+                    row = jnp.where(lane == c * SLOTS + k, q, row)
+            sidx[m] = row
+
+    idx_in[0, 0] = sidx[0]
 
     @pl.loop(0, 16)
     def _(i):
         for j in range(4):
             c = i * 4 + j
             wtd[c] = (area[pl.ds(c, 1), :] * rad[c].astype(jnp.float32)).astype(jnp.bfloat16)
+
+    pl.semaphore_wait(barrier, DEV - 1)
+
+    core = me[3]
+
+    def idx_copy(rows, m):
+        z2, g2 = chip(me, m)
+        return pltpu.make_async_remote_copy(
+            src_ref=sidx.at[rows], dst_ref=idx_in.at[0, rows], send_sem=idx_send, recv_sem=idx_recv,
+            device_id=(z2, g2 + core), device_id_type=MESH,
+        )
+
+    def pair_copy():
+        z2, g2 = chip(me, 0)
+        return pltpu.make_async_remote_copy(
+            src_ref=idx_in.at[0], dst_ref=idx_in.at[1], send_sem=pair_send, recv_sem=pair_recv,
+            device_id=(z2, g2 + 1 - core), device_id_type=MESH,
+        )
+
+    for m in range(1, 3):
+        idx_copy(m, m).start()
+
+    @pl.loop(1, 21)
+    def _(i):
+        for j in range(3):
+            m = i * 3 + j
+            idx_copy(m, m).start()
+
+    idx_copy(63, 63).start()
 
     def bwd_copy(first, count, s, c):
         return pltpu.make_async_remote_copy(
@@ -133,14 +178,18 @@
 
     def rad_copy(rows, s, c):
         return pltpu.make_async_remote_copy(
-            src_ref=srad.at[rows], dst_ref=rrad.at[rows], send_sem=rad_send,
+            src_ref=srad.at[rows], dst_ref=rrad.at[rows], send_sem=rad_send.at[c],
             recv_sem=rad_recv.at[c], device_id=peer(me, s, -1), device_id_type=MESH,
         )
 
-    def send_rad(g, first=0):
+    def rad_rest(c):
+        first = max(1, c * PER)
+        return rad_copy(pl.ds(first, (c + 1) * PER - first), 1, c)
+
+    def send_rad(g, c, first=0):
         for j in range(first, GRP):
             s = g * GRP + j
-            rad_copy(s, s, lax.div(s, PER)).start()
+            rad_copy(s, s, c).start()
 
     def send_bwd(g, c, first=0):
         for j in range(first, GRP):
@@ -192,78 +241,102 @@
             bwd_group(g)
             send_bwd(g - 1, c)
 
+    others = pl.ds(1, 63)
+    idx_copy(others, 1).wait()
+    pair_copy().start()
+
+    for k in range(SLOTS):
+        bwd_0[0, k] = sbwd[0, k]
+
+    pair_copy().wait()
+    weight = jnp.zeros((1, 128), jnp.int32)
+    for k in range(SLOTS):
+        weight = jnp.where(lane == core * SLOTS + k, 128**k, weight)
+
+    def rad_group(g):
+        for j in range(GRP):
+            s = g * GRP + j
+            oc, m = index_spot(s)
+            packed = jnp.sum(idx_in[oc, m] * weight)
+            for k in range(SLOTS):
+                srad[s, k] = rad[lax.rem(lax.div(packed, 128**k), 64)]
+
+    rad_group(0)
+    rad_group(1)
+    send_rad(0, 0, 1)
+
+    @pl.loop(2, lap + 1)
+    def _(g):
+        rad_group(g)
+        send_rad(g - 1, 0)
+
+    for c in range(1, CHUNKS):
+
+        @pl.loop(c * lap + 1, min((c + 1) * lap + 1, GROUPS))
+        def _(g):
+            rad_group(g)
+            send_rad(g - 1, c)
+
+    for k in range(SLOTS):
+        rrad[0, k] = srad[0, k]
+    send_rad(GROUPS - 1, CHUNKS - 1)
+
+
     @pl.loop(EARLY * lap + 1, GROUPS)
     def _(g):
         bwd_group(g)
 
-    fill(tidx, tgt_s)
-
-    for k in range(SLOTS):
-        bwd_0[0, k] = sbwd[0, k]
-
-    rest = pl.ds(1, DEV - 1)
-    idx_copy(rest, 1).wait()
-    to_smem = pltpu.make_async_copy(idx_in, idx_s, msem.at[0])
-    to_smem.start()
-    to_smem.wait()
-
-    def rad_group(g):
-        for j in range(GRP):
-            s = g * GRP + j
-            for k in range(SLOTS):
-                srad[s, k] = rad[lax.rem(idx_s[s, 0, k], 64)]
-
-    rad_group(0)
-    rad_group(1)
-    send_rad(0, 1)
-
-    @pl.loop(2, GROUPS)
-    def _(g):
-        rad_group(g)
-        send_rad(g - 1)
-
-    for k in range(SLOTS):
-        rrad[0, k] = srad[0, k]
-    send_rad(GROUPS - 1)
-
-    for c in range(EARLY, CHUNKS):
-
-        @pl.loop(c * lap, (c + 1) * lap)
-        def _(g):
-            send_bwd(g, c)
-
-    def order(ids, c, base):
+
+    def order(ids, which, c, base):
         block = ids[pl.ds(c * PER, PER)].reshape(PER, 128)
-        q = jnp.concatenate(
-            [jnp.broadcast_to(block[:, k : k + 1], (PER, 128)) for k in range(SLOTS)], axis=0
-        )
+        parts = []
+        for k in range(SLOTS):
+            low = block[:, k : k + 1]
+            high = block[:, SLOTS + k : SLOTS + k + 1]
+            parts.append(jnp.broadcast_to(low + which * (high - low), (PER, 128)))
+        q = jnp.concatenate(parts, axis=0)
         lanes = lax.broadcasted_iota(jnp.int32, (128, 128), 1)
         key = q * 128 + lax.broadcasted_iota(jnp.int32, (128, 128), 0)
         rank = jnp.sum((key.T < key).astype(jnp.int32), axis=1, keepdims=True)
-        meta_v[base + 2 * c] = jnp.sum(jnp.where(rank == lanes, key, 0), axis=0, keepdims=True)
+        meta_v[base, 2 * c] = jnp.sum(jnp.where(rank == lanes, key, 0), axis=0, keepdims=True)
         upto = jnp.sum((q <= lanes).astype(jnp.int32), axis=0, keepdims=True)
         below = jnp.sum((q < lanes).astype(jnp.int32), axis=0, keepdims=True)
-        meta_v[base + 2 * c + 1] = jnp.where(upto > below, upto, 0)
+        meta_v[base, 2 * c + 1] = jnp.where(upto > below, upto, 0)
+
+    def meta_copy(i):
+        return pltpu.make_async_copy(meta_v.at[i], meta_s.at[i], msem.at[i])
+
+    fill(tidx, tgt_s)
 
     @pl.loop(0, CHUNKS)
     def _(c):
-        order(tidx, c, 0)
-        order(idx_in, c, 2 * CHUNKS)
-
-    to_smem = pltpu.make_async_copy(meta_v, meta_s, msem.at[1])
-    to_smem.start()
-    to_smem.wait()
+        order(tidx, 0, c, 0)
+
+    meta_copy(0).start()
+
+    @pl.loop(0, GROUPS)
+    def _(g):
+        for j in range(GRP):
+            s = g * GRP + j
+            oc, m = index_spot(s)
+            ridx[s] = idx_in[oc, m]
+
+    @pl.loop(0, CHUNKS)
+    def _(c):
+        order(ridx, core, c, 1)
+
+    meta_copy(1).start()
 
     seq[0] = jnp.zeros((16, 128), jnp.float32)
     gat[...] = jnp.zeros_like(gat)
     ret[...] = jnp.zeros_like(ret)
 
-    def scan(values, offset, total, c, base):
+    def scan(values, offset, finish, c, base):
         def body(i, carry):
             acc, last = carry
             for j in range(8):
                 n = i * 8 + j
-                key = meta_s[base + 2 * c, 0, n]
+                key = meta_s[base, 2 * c, 0, n]
                 q = lax.div(key, 128)
                 item = lax.rem(key, 128)
                 x = values[offset + lax.rem(item, PER), lax.div(item, PER)].astype(jnp.float32)
@@ -278,29 +351,48 @@
         def _(i):
             for j in range(4):
                 t = i * 4 + j
-                total[t] += seq[meta_s[base + 2 * c + 1, 0, t]]
+                finish(t, seq[meta_s[base, 2 * c + 1, 0, t]])
+
+    def to_gat(t, part):
+        gat[t] += part
+
+    def to_ret(t, part):
+        ret[t] += part
+
+    def to_irr(t, part):
+        irr[t] = gat[t] + (ret[t] + part) / area[pl.ds(t, 1), :]
+
+    meta_copy(0).wait()
 
     for c in range(CHUNKS):
-        first = max(1, c * PER)
-        rad_copy(pl.ds(first, (c + 1) * PER - first), 1, c).wait_recv()
+        rad_rest(c).wait_recv()
 
         @pl.loop(c * lap, (c + 1) * lap)
         def _(g):
             fwd_group(g)
 
-        scan(fwd, c * PER, gat, c, 0)
+        scan(fwd, c * PER, to_gat, c, 0)
+
+        if EARLY + c < CHUNKS:
+
+            @pl.loop((EARLY + c) * lap, (EARLY + c + 1) * lap)
+            def _(g):
+                send_bwd(g, EARLY + c)
+
+    meta_copy(1).wait()
 
     for c in range(CHUNKS):
         bwd_rest(c).wait_recv()
-        scan(bwd_in[c], 0, ret, c, 2 * CHUNKS)
-
-    @pl.loop(0, 64)
-    def _(c):
-        irr[c] = gat[c] + ret[c] / area[pl.ds(c, 1), :]
-
-    for c in range(CHUNKS):
-        bwd_rest(c).wait_send()
-    rad_copy(rest, 1, 0).wait_send()
+        scan(bwd_in[c], 0, to_ret if c < CHUNKS - 1 else to_irr, c, 1)
+
+    bwd_rest(0).wait_send()
+    bwd_rest(1).wait_send()
+    bwd_rest(2).wait_send()
+    bwd_rest(3).wait_send()
+    rad_rest(0).wait_send()
+    rad_rest(1).wait_send()
+    rad_rest(2).wait_send()
+    rad_rest(3).wait_send()
 
 
 def shards(
@@ -331,16 +423,16 @@
             pltpu.VMEM(slab, jnp.bfloat16),
             pltpu.VMEM(slab, jnp.bfloat16),
             pltpu.VMEM(slab, jnp.float32),
-            pltpu.VMEM(rows, jnp.int32),
+            pltpu.VMEM((64, 1, 128), jnp.int32),
+            pltpu.VMEM((2, 64, 1, 128), jnp.int32),
             pltpu.VMEM(rows, jnp.int32),
             pltpu.VMEM(rows, jnp.int32),
             pltpu.VMEM((136, 16, 128), jnp.float32),
             pltpu.VMEM((64, 16, 128), jnp.float32),
             pltpu.VMEM((64, 16, 128), jnp.float32),
-            pltpu.VMEM((4 * CHUNKS, 1, 128), jnp.int32),
-            pltpu.SMEM(rows, jnp.int32),
-            pltpu.SMEM((4 * CHUNKS, 1, 128), jnp.int32),
-            dma((6,)), dma((FCH,)), dma((2,)), dma, dma, dma((CHUNKS,)), dma((CHUNKS,)), dma, dma((CHUNKS,)),
+            pltpu.VMEM((2, 2 * CHUNKS, 1, 128), jnp.int32),
+            pltpu.SMEM((2, 2 * CHUNKS, 1, 128), jnp.int32),
+            dma((6,)), dma((FCH,)), dma((2,)), dma, dma, dma, dma, dma((CHUNKS,)), dma((CHUNKS,)), dma((CHUNKS,)), dma((CHUNKS,)),
         ],
         compiler_params=pltpu.CompilerParams(
             collective_id=0, has_side_effects=True, vmem_limit_bytes=48 << 20

time: 72.7 us -> 67.1 us (0.923)
  the two profiles are of different devices: /device:TPU:1 before, /device:TPU:65 now
where the time goes in v4:
time: 67.1 us; the launch traced here: 67 us
  Pallas kernels  66.1 us (99%)
  other arithmetic  0.89 us (1%)
    pallas_call x1, Pallas kernels, shards(): pl.pallas_call(exchange_kernel, out_shape=jax.ShapeDtypeStruct((64, 16, 1...  66.1 us

profile of v4, /device:TPU:65, one launch (start us, length us, event | category | flops | bytes accessed | tf_op | source)
XLA Modules:
  0.0 67.0 jit_solution(10311157074836585626)
XLA Ops:
  0.0 0.0 copy-start.1
  0.0 0.0 copy-start
  0.0 66.1 %exchange.1 = f32[64,16,128]{2,1,0:T(8,128)S(1)} custom-call(s32[1,512]{1,0:T(1,128)} %src_h.1, s32[1,512]{1,0:T(1,128)} %tgt_h.1, s32[1,512]{1,0:T(1,128)} %blk_h.1, s32[1,128]{1,0:T(1,128)} %val_h.1, bf16[64,16,128]{2,1,0:T(8,128)(2,1)} %rad_h.1, f32[64,128]{1,0:T(8,128)} %area_h.1, bf16[512,128,128]{2,1,0:T(8,128)(2,1)} %f_h.1), custom_call_target="tpu_custom_call" | custom-call | tf_op jit(solution)/shard_map/exchange/pallas_call | solution.py:407
  66.1 0.0 copy-done.1
  66.1 0.0 copy-done
  66.1 0.9 %multiply_add_fusion = f32[64,16,128]{2,1,0:T(8,128)} fusion(f32[64,16,128]{2,1,0:T(8,128)S(1)} %copy-done, f32[64,16,128]{2,1,0:T(8,128)S(1)} %copy-done.1, f32[64,16,128]{2,1,0:T(8,128)S(1)} %exchange.1), kind=kLoop, calls=%fused_computation | loop fusion | flops 262144 | bytes 2097152 | tf_op jit(solution)/shard_map/add | solution.py:444
Async XLA Ops:
  0.0 66.1 %copy-start.1 = (f32[64,16,128]{2,1,0:T(8,128)S(1)}, f32[64,16,128]{2,1,0:T(8,128)}, u32[]{:S(2)}) copy-start(f32[64,16,128]{2,1,0:T(8,128)} %param.11) | copy-start | bytes 1572868
  0.0 66.1 %copy-start = (f32[64,16,128]{2,1,0:T(8,128)S(1)}, f32[64,16,128]{2,1,0:T(8,128)}, u32[]{:S(2)}) copy-start(f32[64,16,128]{2,1,0:T(8,128)} %param.10) | copy-start | bytes 1572868

commit v5 on v4

--- a/solution.py
+++ b/solution.py
@@ -259,7 +259,7 @@
             oc, m = index_spot(s)
             packed = jnp.sum(idx_in[oc, m] * weight)
             for k in range(SLOTS):
-                srad[s, k] = rad[lax.rem(lax.div(packed, 128**k), 64)]
+                srad[s, k] = rad[jnp.bitwise_and(jnp.right_shift(packed, 7 * k), 63)]
 
     rad_group(0)
     rad_group(1)
@@ -286,6 +286,12 @@
     def _(g):
         bwd_group(g)
 
+
+    for c in range(EARLY, CHUNKS):
+
+        @pl.loop(c * lap, (c + 1) * lap)
+        def _(g):
+            send_bwd(g, c)
 
     def order(ids, which, c, base):
         block = ids[pl.ds(c * PER, PER)].reshape(PER, 128)
@@ -337,9 +343,11 @@
             for j in range(8):
                 n = i * 8 + j
                 key = meta_s[base, 2 * c, 0, n]
-                q = lax.div(key, 128)
-                item = lax.rem(key, 128)
-                x = values[offset + lax.rem(item, PER), lax.div(item, PER)].astype(jnp.float32)
+                q = jnp.right_shift(key, 7)
+                item = jnp.bitwise_and(key, 127)
+                row = jnp.bitwise_and(item, PER - 1)
+                slot = jnp.right_shift(item, 5)
+                x = values[offset + row, slot].astype(jnp.float32)
                 acc = acc * jnp.where(q == last, 1.0, 0.0) + x
                 seq[n + 1] = acc
                 last = q
@@ -372,12 +380,6 @@
             fwd_group(g)
 
         scan(fwd, c * PER, to_gat, c, 0)
-
-        if EARLY + c < CHUNKS:
-
-            @pl.loop((EARLY + c) * lap, (EARLY + c + 1) * lap)
-            def _(g):
-                send_bwd(g, EARLY + c)
 
     meta_copy(1).wait()
 

time: 67.1 us -> 65.5 us (0.976)
  the two profiles are of different devices: /device:TPU:65 before, /device:TPU:1 now
where the time goes in v5:
time: 65.5 us; the launch traced here: 65 us
  Pallas kernels  64 us (98%)
  other arithmetic  0.89 us (1%)
    pallas_call x1, Pallas kernels, shards(): pl.pallas_call(exchange_kernel, out_shape=jax.ShapeDtypeStruct((64, 16, 1...  64 us

profile of v5, /device:TPU:1, one launch (start us, length us, event | category | flops | bytes accessed | tf_op | source)
XLA Modules:
  0.0 65.0 jit_solution(3899775704468263865)
XLA Ops:
  0.0 0.0 copy-start.1
  0.0 0.0 copy-start
  0.0 64.0 %exchange.1 = f32[64,16,128]{2,1,0:T(8,128)S(1)} custom-call(s32[1,512]{1,0:T(1,128)} %src_h.1, s32[1,512]{1,0:T(1,128)} %tgt_h.1, s32[1,512]{1,0:T(1,128)} %blk_h.1, s32[1,128]{1,0:T(1,128)} %val_h.1, bf16[64,16,128]{2,1,0:T(8,128)(2,1)} %rad_h.1, f32[64,128]{1,0:T(8,128)} %area_h.1, bf16[512,128,128]{2,1,0:T(8,128)(2,1)} %f_h.1), custom_call_target="tpu_custom_call" | custom-call | tf_op jit(solution)/shard_map/exchange/pallas_call | solution.py:409
  64.1 0.0 copy-done.1
  64.1 0.0 copy-done
  64.1 0.9 %multiply_add_fusion = f32[64,16,128]{2,1,0:T(8,128)} fusion(f32[64,16,128]{2,1,0:T(8,128)S(1)} %copy-done, f32[64,16,128]{2,1,0:T(8,128)S(1)} %copy-done.1, f32[64,16,128]{2,1,0:T(8,128)S(1)} %exchange.1), kind=kLoop, calls=%fused_computation | loop fusion | flops 262144 | bytes 2097152 | tf_op jit(solution)/shard_map/add | solution.py:446
Async XLA Ops:
  0.0 64.1 %copy-start.1 = (f32[64,16,128]{2,1,0:T(8,128)S(1)}, f32[64,16,128]{2,1,0:T(8,128)}, u32[]{:S(2)}) copy-start(f32[64,16,128]{2,1,0:T(8,128)} %param.11) | copy-start | bytes 1572868
  0.0 64.1 %copy-start = (f32[64,16,128]{2,1,0:T(8,128)S(1)}, f32[64,16,128]{2,1,0:T(8,128)}, u32[]{:S(2)}) copy-start(f32[64,16,128]{2,1,0:T(8,128)} %param.10) | copy-start | bytes 1572868

commit v6 on v5

--- a/solution.py
+++ b/solution.py
@@ -13,7 +13,7 @@
 EARLY = 2
 CHUNKS = 4
 PER = DEV // CHUNKS
-FCH = 8
+FCH = 2
 MIX = 13
 
 

time: 65.5 us -> 64.6 us (0.986)
  no operation moved by 1% of the time
where the time goes in v6:
time: 64.6 us; the launch traced here: 64.5 us
  Pallas kernels  63.5 us (98%)
  other arithmetic  0.89 us (1%)
    pallas_call x1, Pallas kernels, shards(): pl.pallas_call(exchange_kernel, out_shape=jax.ShapeDtypeStruct((64, 16, 1...  63.5 us

profile of v6, /device:TPU:1, one launch (start us, length us, event | category | flops | bytes accessed | tf_op | source)
XLA Modules:
  0.0 64.5 jit_solution(6996047622748374866)
XLA Ops:
  0.0 0.0 copy-start.1
  0.0 0.0 copy-start
  0.0 63.5 %exchange.1 = f32[64,16,128]{2,1,0:T(8,128)S(1)} custom-call(s32[1,512]{1,0:T(1,128)} %src_h.1, s32[1,512]{1,0:T(1,128)} %tgt_h.1, s32[1,512]{1,0:T(1,128)} %blk_h.1, s32[1,128]{1,0:T(1,128)} %val_h.1, bf16[64,16,128]{2,1,0:T(8,128)(2,1)} %rad_h.1, f32[64,128]{1,0:T(8,128)} %area_h.1, bf16[512,128,128]{2,1,0:T(8,128)(2,1)} %f_h.1), custom_call_target="tpu_custom_call" | custom-call | tf_op jit(solution)/shard_map/exchange/pallas_call | solution.py:409
  63.6 0.0 copy-done.1
  63.6 0.0 copy-done
  63.6 0.9 %multiply_add_fusion = f32[64,16,128]{2,1,0:T(8,128)} fusion(f32[64,16,128]{2,1,0:T(8,128)S(1)} %copy-done, f32[64,16,128]{2,1,0:T(8,128)S(1)} %copy-done.1, f32[64,16,128]{2,1,0:T(8,128)S(1)} %exchange.1), kind=kLoop, calls=%fused_computation | loop fusion | flops 262144 | bytes 2097152 | tf_op jit(solution)/shard_map/add | solution.py:446
Async XLA Ops:
  0.0 63.6 %copy-start.1 = (f32[64,16,128]{2,1,0:T(8,128)S(1)}, f32[64,16,128]{2,1,0:T(8,128)}, u32[]{:S(2)}) copy-start(f32[64,16,128]{2,1,0:T(8,128)} %param.11) | copy-start | bytes 1572868
  0.0 63.6 %copy-start = (f32[64,16,128]{2,1,0:T(8,128)S(1)}, f32[64,16,128]{2,1,0:T(8,128)}, u32[]{:S(2)}) copy-start(f32[64,16,128]{2,1,0:T(8,128)} %param.10) | copy-start | bytes 1572868
